TPU v7x, 512 devices: a whole 4x8x8 slice. The times are simulated.
512 devices in a mesh: dp: 32 (over x, y), mx: 4 (over z_hi, core), my: 4 (over z_lo).
Axes of the slice: x: 4, y: 8, z: 8 (z_hi: 2, z_lo: 4; z = z_hi * 4 + z_lo), core: 2. Of those that a mesh axis runs over, the one named last changes fastest.
Arguments:
- mentor_final_states: bfloat16 [2048, 4608], P('dp'), may hold values from -12 to 12
- mentor_output_matrix: bfloat16 [4608, 4096], P(None, ('mx', 'my')), may hold values from -0.09375 to 0.09375
- learner_final_states: bfloat16 [2048, 3584], P('dp', 'mx'), may hold values from -12 to 12
- learner_output_matrix: bfloat16 [3584, 4096], P('mx', 'my'), may hold values from -0.09375 to 0.09375
- loss_mask: int32 [2048], P('dp'), may hold values 0 or 1
Outputs:
- mismatch_per_piece: float32 [2048], P('dp')
- mean_loss: float32 [], replicated
- student_grad: float32 [2048, 4096], P('dp', 'my')
All inputs are finite; a program needn't handle non-finite values.
Results may differ from a plain program's by a relative error of at most 0.0003.
Values sent between devices are 32-bit elements.
No kernel may reach another device: no remote copies, remote signals or barrier semaphores. Data moves between devices by JAX's collectives and lax.ppermute only.
A program may use at most 64 MiB of HBM per device.

v0:
```python
import jax
import jax.numpy as jnp
from jax import lax
from jax.sharding import Mesh
from jax.sharding import PartitionSpec as P

DP = ("dp_0", "dp_1")
SOFTENING_HEAT = 2.0


def over_axes(array, axes):
    for axis in axes:
        array = lax.psum(array, axis)
    return array


def over_pieces(array, axis):
    blocks = lax.all_gather(array, axis)
    return blocks.sum(axis=0)


def merged(part, axis, combine):
    gathered = jax.tree.map(lambda a: lax.all_gather(a, axis), part)

    def take(source):
        return jax.tree.map(lambda a: lax.dynamic_index_in_dim(a, source, 0, False), gathered)

    return lax.fori_loop(
        1, lax.axis_size(axis), lambda source, state: combine(state, take(source)), take(0)
    )


def picked(array, axis, root):
    return lax.dynamic_index_in_dim(lax.all_gather(array, axis), root, 0, keepdims=False)


def row_stats(values):
    row_max = jnp.max(values, axis=1)
    row_sum = jnp.sum(jnp.exp(values - row_max[:, None]), axis=1)
    return (row_max, row_sum)


def join_stats(left_stat, right_stat):
    row_max = jnp.maximum(left_stat[0], right_stat[0])
    row_sum = left_stat[1] * jnp.exp(left_stat[0] - row_max) + right_stat[1] * jnp.exp(
        right_stat[0] - row_max
    )
    return (row_max, row_sum)


def local(
    mentor_final_states,
    mentor_output_matrix,
    learner_final_states,
    learner_output_matrix,
    loss_mask,
):
    groups = lax.axis_size(("mx", "my"))
    piece_cols = mentor_output_matrix.shape[1]
    lexicon_length = piece_cols * groups
    local_tokens = mentor_final_states.shape[0]
    piece_count = local_tokens * lax.axis_size(DP)
    global_multiplier = SOFTENING_HEAT * lexicon_length * piece_count
    mentor_softened_scores = (
        jnp.dot(mentor_final_states, mentor_output_matrix, preferred_element_type=jnp.float32)
        / SOFTENING_HEAT
    )
    learner_contribution = jnp.dot(
        learner_final_states, learner_output_matrix, preferred_element_type=jnp.float32
    )
    piece_importance = loss_mask.astype(jnp.float32)
    usable_count = over_axes(jnp.sum(piece_importance), DP)
    learner_softened_scores = over_pieces(learner_contribution, "mx") / SOFTENING_HEAT
    teacher_max, teacher_sum = merged(row_stats(mentor_softened_scores), ("mx", "my"), join_stats)
    student_max, student_sum = merged(row_stats(learner_softened_scores), "my", join_stats)
    mentor_logarithmic_odds = mentor_softened_scores - (teacher_max + jnp.log(teacher_sum))[:, None]
    learner_logarithmic_odds = (
        learner_softened_scores - (student_max + jnp.log(student_sum))[:, None]
    )
    outer_block = lax.all_gather(mentor_logarithmic_odds, "my", axis=1, tiled=True)
    aligned = picked(outer_block, "mx", lax.axis_index("my"))
    mentor_likelihoods = jnp.exp(aligned)
    partial_kl = jnp.sum(mentor_likelihoods * (aligned - learner_logarithmic_odds), axis=1)
    mismatch_per_piece = SOFTENING_HEAT * SOFTENING_HEAT * over_pieces(partial_kl, "my")
    prob_gap = jnp.exp(learner_logarithmic_odds) - mentor_likelihoods
    loss_sum = over_axes(jnp.sum(piece_importance * mismatch_per_piece), DP)
    mean_loss = loss_sum / usable_count
    multiplier = piece_importance * global_multiplier / usable_count
    student_grad = prob_gap * multiplier[:, None]
    return (mismatch_per_piece, mean_loss, student_grad)


def solution(mesh):
    split = Mesh(
        mesh.devices.reshape(4, 8, mesh.shape["mx"], mesh.shape["my"]), ("dp_0", "dp_1", "mx", "my")
    )
    in_specs = (P(DP, None), P(None, ("mx", "my")), P(DP, "mx"), P("mx", "my"), P(DP))
    out_specs = (P(DP), P(), P(DP, "my"))
    return jax.shard_map(local, mesh=split, in_specs=in_specs, out_specs=out_specs, check_vma=False)
```

profile of v0, /device:TPU:8, one launch (start us, length us, event | category | flops | bytes accessed | tf_op | source)
XLA Modules:
  0.0 155.5 jit_solution(621932956250404681)
XLA Ops:
  7.2 0.0 copy-start
  7.2 0.0 copy-start.1
  7.2 0.0 all-gather.12.cloned.1.call-start
  7.2 2.9 %fusion.7 = f32[64,1024]{1,0:T(8,128)} fusion(bf16[64,896]{1,0:T(8,128)(2,1)} %param.11, bf16[896,1024]{1,0:T(8,128)(2,1)} %param.12), kind=kOutput, calls=%fused_computation.29 | convolution fusion | flops 117440512 | bytes 2211840 | tf_op jit(solution)/shard_map/dot_general | solution.py:68
  10.1 0.0 all-gather.12.cloned.1.call-update
  10.1 0.0 all-gather.10.cloned.1.call-start
  10.2 0.0 copy-done
  10.2 0.0 copy-done.1
  10.2 0.6 fusion.6
  10.8 0.0 copy-start.2
  10.8 0.2 exponential_reduce_fusion.1
  11.0 1.3 dynamic-slice
  13.0 0.2 dynamic-update-slice
  13.2 0.2 dynamic-update-slice.1
  13.4 40.3 %all-reduce.5 = (f32[1024]{0:T(1024)S(1)}, f32[1024]{0:T(1024)S(1)}) all-reduce(f32[1024]{0:T(1024)S(1)} %dynamic-update-slice, f32[1024]{0:T(1024)S(1)} %dynamic-update-slice.1), channel_id=2, replica_groups=mesh['dp_0'=4,'dp_1'=8,'mx'=4,'my'=4] {'mx','my'}, use_global_device_ids=true, to_apply=%add | all-reduce | flops 2048 | bytes 16384
  53.7 0.1 reshape.11
  53.8 0.1 reshape.12
  53.9 0.7 while.34
  54.5 0.1 broadcast_subtract_fusion
  54.6 15.3 %all_gather.49 = f32[64,1024]{1,0:T(8,128)} all-gather(f32[64,256]{1,0:T(8,128)S(1)} %broadcast_subtract_fusion), channel_id=1, replica_groups=mesh['dp_0'=4,'dp_1'=8,'mx'=4,'my'=4] {'my'}, dimensions={1}, use_global_device_ids=true | all-gather | bytes 327680 | tf_op jit(solution)/shard_map/all_gather | solution.py:80
  69.9 0.0 all-gather.10.cloned.1.call-update
  69.9 1.3 dynamic-slice.2
  71.9 0.0 all-gather.12.cloned.1.call-done
  71.9 1.3 reduce_sum.64
  73.2 0.1 multiply_reduce_fusion
  73.3 0.2 dynamic-update-slice.2
  73.6 0.2 exponential_reduce_fusion
  73.8 0.2 dynamic-update-slice.3
  74.0 8.7 %all-reduce.7 = (f32[256]{0:T(256)S(1)}, f32[256]{0:T(256)S(1)}) all-reduce(f32[256]{0:T(256)S(1)} %dynamic-update-slice.2, f32[256]{0:T(256)S(1)} %dynamic-update-slice.3), channel_id=6, replica_groups=mesh['dp_0'=4,'dp_1'=8,'mx'=4,'my'=4] {'my'}, use_global_device_ids=true, to_apply=%add.2 | all-reduce | flops 512 | bytes 4096
  82.7 0.1 reshape.15
  82.8 0.1 reshape.16
  82.9 0.1 while.35
  83.0 21.3 %all-gather.10.cloned.1.call-done = f32[256,1024]{1,0:T(8,128)} async-done(((f32[64,1024]{1,0:T(8,128)}), f32[256,1024]{1,0:T(8,128)}) %all-gather.10.cloned.1.call-update) | async-done | bytes 1048592 | tf_op jit(solution)/shard_map/all_gather | solution.py:34
  104.4 1.2 fusion.5
  105.5 0.2 dynamic-update-slice.4
  105.8 9.3 %all-reduce.4 = f32[256]{0:T(256)S(1)} all-reduce(f32[256]{0:T(256)S(1)} %dynamic-update-slice.4), channel_id=8, replica_groups=mesh['dp_0'=4,'dp_1'=8,'mx'=4,'my'=4] {'my'}, use_global_device_ids=true, to_apply=%add.4 | all-reduce | flops 256 | bytes 2048
  115.1 0.1 reshape.17
  115.2 0.0 copy-done.2
  115.2 1.1 convert_reduce_fusion
  116.3 11.0 %all-reduce.8 = (f32[]{:T(128)}, f32[]{:T(128)}) all-reduce(f32[]{:T(128)} %get-tuple-element.274, f32[]{:T(128)} %get-tuple-element.273), channel_id=1, replica_groups=mesh['dp_0'=4,'dp_1'=8,'mx'=4,'my'=4] {'dp_0'}, use_global_device_ids=true, to_apply=%region_12.13 | all-reduce | flops 2 | bytes 16 | tf_op jit(solution)/shard_map/psum | solution.py:13
  127.3 16.4 %all-reduce.6 = (f32[]{:T(128)}, f32[]{:T(128)}) all-reduce(f32[]{:T(128)} %get-tuple-element.301, f32[]{:T(128)} %get-tuple-element.302), channel_id=1, replica_groups=mesh['dp_0'=4,'dp_1'=8,'mx'=4,'my'=4] {'dp_1'}, use_global_device_ids=true, to_apply=%region_13.14 | all-reduce | flops 2 | bytes 16 | tf_op jit(solution)/shard_map/psum | solution.py:13
  143.8 0.6 multiply_divide_fusion
  144.4 1.8 %subtract_multiply_fusion = f32[64,1024]{1,0:T(8,128)} fusion(f32[4,64,1024]{2,1,0:T(8,128)} %bitcast.49, s32[]{:T(128)S(6)} %select_n.32, f32[64,1024]{1,0:T(8,128)S(1)} %reduce_sum.64, f32[64]{0:T(128)S(1)} %multiply_divide_fusion, f32[64]{0:T(128)S(1)} %log_add_fusion), kind=kLoop, calls=%fused_computation.17 | loop fusion | flops 262144 | bytes 786948 | tf_op jit(solution)/shard_map/mul | solution.py:89
  (30 shorter events, 0.5 us)
Async XLA Ops:
  7.2 3.0 %copy-start = (bf16[4608,256]{1,0:T(8,128)(2,1)S(1)}, bf16[4608,256]{1,0:T(8,128)(2,1)}, u32[]{:S(2)}) copy-start(bf16[4608,256]{1,0:T(8,128)(2,1)} %param.10) | copy-start | bytes 7077892
  7.2 3.0 %copy-start.1 = (bf16[64,4608]{1,0:T(8,128)(2,1)S(1)}, bf16[64,4608]{1,0:T(8,128)(2,1)}, u32[]{:S(2)}) copy-start(bf16[64,4608]{1,0:T(8,128)(2,1)} %param.9) | copy-start | bytes 1769476
  7.2 64.7 %all-gather.12.cloned.1.call-start = ((), (), s32[]{:S(2)}) async-start(), calls=%async_computation.1 | async-start | bytes 1310720 | tf_op jit(solution)/shard_map/all_gather | solution.py:18
  10.1 94.2 %all-gather.10.cloned.1.call-start = ((), (), s32[]{:S(2)}) async-start(), calls=%async_computation | async-start | bytes 1310720 | tf_op jit(solution)/shard_map/all_gather | solution.py:34
  10.8 104.4 %copy-start.2 = (s32[64]{0:T(128)S(1)}, s32[64]{0:T(128)}, u32[]{:S(2)}) copy-start(s32[64]{0:T(128)} %param.13) | copy-start | bytes 772
Sparse Core Ops, SparseCore 0:
  10.7 39.8 all-gather.11
  70.1 34.2 all-gather.9
where the time goes:
time: 156 us
  blocking collectives  101 us (65%)
  waiting for transfers between devices  21.4 us (14%)
  between operations  18 us (12%)
  other arithmetic  7.11 us (5%)
  local copies, waits for them, and re-layouts  4.15 us (3%)
  matrix products  3.48 us (2%)
    unnamed x3, blocking collectives  58.3 us
    psum x2, blocking collectives, over_axes(): array = lax.psum(array, axis)  27.4 us
    all_gather x1, waiting for transfers between devices, picked(): lax.all_gather(array, axis)  21.3 us
    all_gather x1, blocking collectives, local(): lax.all_gather(mentor_logarithmic_odds, 'my', axis=1, tiled=True)  15.3 us
    unnamed x18, local copies, waits for them, and re-layouts  3.76 us
  transfers between devices with their start and end apart: 2, of which 1 were waited for; matrix products, arithmetic and copies ran while one was open for 4% of the time, Pallas kernels for 0%

commit v1 on v0

--- a/solution.py
+++ b/solution.py
@@ -10,7 +10,8 @@
 
 def over_axes(array, axes):
     for axis in axes:
-        array = lax.psum(array, axis)
+        parts = lax.all_gather(array, axis)
+        array = jnp.sum(parts, axis=0)
     return array
 
 

time: 156 us -> 164 us (1.051)
  local copies, waits for them, and re-layouts: 4.15 us -> 12.2 us
  other arithmetic: 7.11 us -> 9.71 us
    psum x2 -> x0, blocking collectives: 27.4 us -> none  [over_axes(): array = lax.psum(array, axis)]
    unnamed x3 -> x5, blocking collectives: 58.3 us -> 84.7 us
    unnamed x18 -> x28, local copies, waits for them, and re-layouts: 3.76 us -> 11.8 us
    reduce_sum x0 -> x4, other arithmetic: none -> 2.56 us  [over_axes(): array = jnp.sum(parts, axis=0)]
  transfers between devices with their start and end apart: 2 -> 2, of which waited for: 1 -> 1; matrix products, arithmetic and copies ran while one was open for 4% -> 5% of each run, Pallas kernels for 0% -> 0%
where the time goes in v1:
time: 164 us
  blocking collectives  99.8 us (61%)
  waiting for transfers between devices  20 us (12%)
  between operations  18 us (11%)
  local copies, waits for them, and re-layouts  12.2 us (7%)
  other arithmetic  9.71 us (6%)
  matrix products  3.48 us (2%)
    unnamed x5, blocking collectives  84.7 us
    all_gather x1, waiting for transfers between devices, picked(): lax.all_gather(array, axis)  20 us
    all_gather x1, blocking collectives, local(): lax.all_gather(mentor_logarithmic_odds, 'my', axis=1, tiled=True)  15.1 us
    unnamed x28, local copies, waits for them, and re-layouts  11.8 us
  transfers between devices with their start and end apart: 2, of which 1 were waited for; matrix products, arithmetic and copies ran while one was open for 5% of the time, Pallas kernels for 0%

profile of v1, /device:TPU:8, one launch (start us, length us, event | category | flops | bytes accessed | tf_op | source)
XLA Modules:
  0.0 163.6 jit_solution(7547707529276238383)
XLA Ops:
  7.2 0.0 copy-start
  7.2 0.0 copy-start.1
  7.2 0.0 all-gather.12.cloned.1.call-start
  7.2 2.9 %fusion.7 = f32[64,1024]{1,0:T(8,128)} fusion(bf16[64,896]{1,0:T(8,128)(2,1)} %param.11, bf16[896,1024]{1,0:T(8,128)(2,1)} %param.12), kind=kOutput, calls=%fused_computation.29 | convolution fusion | flops 117440512 | bytes 2211840 | tf_op jit(solution)/shard_map/dot_general | solution.py:69
  10.1 0.0 all-gather.12.cloned.1.call-update
  10.1 0.0 all-gather.10.cloned.1.call-start
  10.2 1.3 dynamic-slice
  12.1 0.0 copy-done
  12.1 0.0 copy-done.1
  12.1 0.6 fusion.6
  12.7 0.0 copy-start.2
  12.8 0.2 exponential_reduce_fusion.1
  12.9 0.2 dynamic-update-slice
  13.2 0.2 dynamic-update-slice.1
  13.4 40.3 %all-reduce.9 = (f32[1024]{0:T(1024)S(1)}, f32[1024]{0:T(1024)S(1)}) all-reduce(f32[1024]{0:T(1024)S(1)} %dynamic-update-slice, f32[1024]{0:T(1024)S(1)} %dynamic-update-slice.1), channel_id=2, replica_groups=mesh['dp_0'=4,'dp_1'=8,'mx'=4,'my'=4] {'mx','my'}, use_global_device_ids=true, to_apply=%add | all-reduce | flops 2048 | bytes 16384
  53.7 0.1 reshape.11
  53.8 0.1 reshape.12
  53.9 0.7 while.34
  54.6 0.1 broadcast_subtract_fusion
  54.6 15.1 %all_gather.73 = f32[64,1024]{1,0:T(8,128)} all-gather(f32[64,256]{1,0:T(8,128)S(1)} %broadcast_subtract_fusion), channel_id=1, replica_groups=mesh['dp_0'=4,'dp_1'=8,'mx'=4,'my'=4] {'my'}, dimensions={1}, use_global_device_ids=true | all-gather | bytes 327680 | tf_op jit(solution)/shard_map/all_gather | solution.py:81
  69.8 0.0 all-gather.10.cloned.1.call-update
  69.8 1.3 dynamic-slice.2
  71.7 1.3 dynamic-slice.5
  73.0 0.0 all-gather.12.cloned.1.call-done
  73.0 1.3 reduce_sum.100
  74.3 0.1 multiply_reduce_fusion
  74.4 0.2 dynamic-update-slice.2
  74.7 0.2 exponential_reduce_fusion
  74.9 0.2 dynamic-update-slice.3
  75.1 9.0 %all-reduce.11 = (f32[256]{0:T(256)S(1)}, f32[256]{0:T(256)S(1)}) all-reduce(f32[256]{0:T(256)S(1)} %dynamic-update-slice.2, f32[256]{0:T(256)S(1)} %dynamic-update-slice.3), channel_id=6, replica_groups=mesh['dp_0'=4,'dp_1'=8,'mx'=4,'my'=4] {'my'}, use_global_device_ids=true, to_apply=%add.2 | all-reduce | flops 512 | bytes 4096
  84.1 0.1 reshape.15
  84.2 0.1 reshape.16
  84.2 0.1 while.35
  84.4 20.0 %all-gather.10.cloned.1.call-done = f32[256,1024]{1,0:T(8,128)} async-done(((f32[64,1024]{1,0:T(8,128)}), f32[256,1024]{1,0:T(8,128)}) %all-gather.10.cloned.1.call-update) | async-done | bytes 1048592 | tf_op jit(solution)/shard_map/all_gather | solution.py:35
  104.4 1.2 fusion.5
  105.5 0.2 dynamic-update-slice.4
  105.8 9.3 %all-reduce.4 = f32[256]{0:T(256)S(1)} all-reduce(f32[256]{0:T(256)S(1)} %dynamic-update-slice.4), channel_id=8, replica_groups=mesh['dp_0'=4,'dp_1'=8,'mx'=4,'my'=4] {'my'}, use_global_device_ids=true, to_apply=%add.4 | all-reduce | flops 256 | bytes 2048
  115.1 0.1 reshape.17
  115.2 0.0 copy-done.2
  115.2 1.1 convert_reduce_fusion
  116.3 1.3 dynamic-update-slice.7
  117.6 1.3 dynamic-update-slice.5
  119.0 1.3 dynamic-slice.6
  120.2 10.4 %all-reduce.12 = (f32[4]{0:T(128)S(1)}, f32[4]{0:T(128)S(1)}) all-reduce(f32[4]{0:T(128)S(1)} %dynamic-update-slice.5, f32[4]{0:T(128)S(1)} %dynamic-update-slice.7), channel_id=1, replica_groups=mesh['dp_0'=4,'dp_1'=8,'mx'=4,'my'=4] {'dp_0'}, use_global_device_ids=true, to_apply=%add.5 | all-reduce | flops 8 | bytes 64
  130.6 0.7 reduce_sum.108
  131.3 0.6 reduce_sum.105
  131.9 1.4 dynamic-update-slice.8
  133.3 1.4 dynamic-update-slice.6
  134.7 15.7 %all-reduce.10 = (f32[8]{0:T(128)S(1)}, f32[8]{0:T(128)S(1)}) all-reduce(f32[8]{0:T(128)S(1)} %dynamic-update-slice.6, f32[8]{0:T(128)S(1)} %dynamic-update-slice.8), channel_id=1, replica_groups=mesh['dp_0'=4,'dp_1'=8,'mx'=4,'my'=4] {'dp_1'}, use_global_device_ids=true, to_apply=%add.6 | all-reduce | flops 16 | bytes 128
  150.5 0.7 reduce_sum.109
  151.1 0.7 multiply_divide_fusion
  151.8 1.8 %subtract_multiply_fusion = f32[64,1024]{1,0:T(8,128)} fusion(f32[4,64,1024]{2,1,0:T(8,128)} %bitcast.55, s32[]{:T(128)S(6)} %select_n.32, f32[64,1024]{1,0:T(8,128)S(1)} %reduce_sum.100, f32[64]{0:T(128)S(1)} %multiply_divide_fusion, f32[64]{0:T(128)S(1)} %log_add_fusion), kind=kLoop, calls=%fused_computation.17 | loop fusion | flops 262144 | bytes 786948 | tf_op jit(solution)/shard_map/mul | solution.py:90
  153.6 0.6 reduce_sum.106
  (34 shorter events, 0.5 us)
Async XLA Ops:
  7.2 4.9 %copy-start = (bf16[4608,256]{1,0:T(8,128)(2,1)S(1)}, bf16[4608,256]{1,0:T(8,128)(2,1)}, u32[]{:S(2)}) copy-start(bf16[4608,256]{1,0:T(8,128)(2,1)} %param.10) | copy-start | bytes 7077892
  7.2 4.9 %copy-start.1 = (bf16[64,4608]{1,0:T(8,128)(2,1)S(1)}, bf16[64,4608]{1,0:T(8,128)(2,1)}, u32[]{:S(2)}) copy-start(bf16[64,4608]{1,0:T(8,128)(2,1)} %param.9) | copy-start | bytes 1769476
  7.2 65.8 %all-gather.12.cloned.1.call-start = ((), (), s32[]{:S(2)}) async-start(), calls=%async_computation.1 | async-start | bytes 1310720 | tf_op jit(solution)/shard_map/all_gather | solution.py:19
  10.1 94.3 %all-gather.10.cloned.1.call-start = ((), (), s32[]{:S(2)}) async-start(), calls=%async_computation | async-start | bytes 1310720 | tf_op jit(solution)/shard_map/all_gather | solution.py:35
  12.7 102.5 %copy-start.2 = (s32[64]{0:T(128)S(1)}, s32[64]{0:T(128)}, u32[]{:S(2)}) copy-start(s32[64]{0:T(128)} %param.13) | copy-start | bytes 772
Sparse Core Ops, SparseCore 0:
  10.7 39.8 all-gather.11
  69.9 34.4 all-gather.9
